TPU v7x, 32 devices: a whole 2x2x4 slice. The times are simulated.
32 devices in a mesh: shot: 4 (over x, core), tile: 8 (over z, y).
Axes of the slice: x: 2, y: 2, z: 4, core: 2. Of those that a mesh axis runs over, the one named last changes fastest.
Arguments:
- partials: bfloat16 [32, 8, 512, 512], P(('shot', 'tile')), may hold values from -6 to 6
Outputs:
- filtered: float32 [8, 512, 512], P('shot', 'tile')
All inputs are finite; a program needn't handle non-finite values.
Results may differ from a plain program's by a relative error of at most 0.0003.
Values may be sent and summed in bfloat16 or wider, within the bound.
A program may use at most 64 MiB of HBM per device.

v0:
```python
import jax
import jax.numpy as jnp
from jax import lax
from jax.sharding import PartitionSpec as P


def padded_2(cells, sides, width):
    for axis, dim in sides:
        count = lax.axis_size(axis)
        ends = count - 1
        head = lax.slice_in_dim(cells, 0, width, axis=dim)
        tail = lax.slice_in_dim(cells, cells.shape[dim] - width, cells.shape[dim], axis=dim)
        cells = jnp.concatenate(
            [
                lax.ppermute(tail, axis, [(i, (i + 1) % count) for i in range(ends)]),
                cells,
                lax.ppermute(head, axis, [((i + 1) % count, i) for i in range(ends)]),
            ],
            axis=dim,
        )
    return cells


def body(partials):
    groups = lax.axis_size("shot")
    members = lax.axis_size("tile")
    depth_all = partials.shape[1]
    depth_part = depth_all // groups
    moved = lax.all_to_all(partials, "tile", split_axis=2, concat_axis=0, tiled=True)
    strip = jnp.sum(moved, axis=0, dtype=jnp.float32)
    full = lax.psum(strip, "shot")
    offset = lax.axis_index("shot") * depth_part
    block = lax.dynamic_slice_in_dim(full, offset, depth_part, 0)
    image = block / jnp.sqrt(jnp.float32(groups * members))
    padded = padded_2(image, (("shot", 0), ("tile", 1)), 1)
    padded = jnp.pad(padded, ((0, 0), (0, 0), (1, 1)))
    beside = padded[2:, 1:-1, 1:-1] + padded[:-2, 1:-1, 1:-1]
    beside = beside + padded[1:-1, 2:, 1:-1] + padded[1:-1, :-2, 1:-1]
    beside = beside + padded[1:-1, 1:-1, 2:] + padded[1:-1, 1:-1, :-2]
    return 6.0 * image - beside


def solution(mesh):
    return jax.shard_map(
        body,
        mesh=mesh,
        in_specs=(P(("shot", "tile"), None, None, None),),
        out_specs=P("shot", "tile", None),
        check_vma=False,
    )
```

profile of v0, /device:TPU:10, one launch (start us, length us, event | category | flops | bytes accessed | tf_op | source)
XLA Modules:
  0.0 177.2 jit_solution(8286965330492240074)
XLA Ops:
  6.5 0.0 all-reduce.3.cloned.1.call-start
  6.5 4.5 %copy.3 = bf16[1,8,512,512]{3,1,0,2:T(8,128)(2,1)S(1)} copy(bf16[1,8,512,512]{3,2,1,0:T(8,128)(2,1)} %param.1) | data formatting | bytes 8388608 | tf_op args[0]
  11.1 98.3 %all_to_all.4 = bf16[1,8,512,512]{3,1,0,2:T(8,128)(2,1)S(1)} all-to-all(bf16[1,8,512,512]{3,1,0,2:T(8,128)(2,1)S(1)} %copy.3), channel_id=1, replica_groups=mesh['shot'=4,'tile'=8] {'tile'}, dimensions={2} | all-to-all | bytes 8388608 | tf_op jit(solution)/shard_map/all_to_all | solution.py:29
  109.4 1.6 convert_reduce_fusion
  111.0 0.0 all-reduce.3.cloned.1.call-update
  111.0 35.4 %all-reduce.3.cloned.1.call-done = f32[8,64,512]{2,0,1:T(8,128)} async-done(((f32[8,64,512]{2,0,1:T(8,128)}), f32[8,64,512]{2,0,1:T(8,128)}) %all-reduce.3.cloned.1.call-update) | async-done | bytes 1048592 | tf_op jit(solution)/shard_map/psum | solution.py:31
  146.4 1.4 dynamic-slice_multiply_fusion
  147.8 0.2 fusion.5
  148.0 1.9 %collective-permute-start = (f32[1,64,512]{2,0,1:T(1,128)S(1)}, f32[1,64,512]{2,0,1:T(1,128)S(1)}, u32[]{:S(2)}, u32[]{:S(2)}) collective-permute-start(f32[1,64,512]{2,0,1:T(1,128)S(1)} %get-tuple-element.8), channel_id=1, source_target_pairs={{8,0},{16,8},{24,16},{9,1},{17,9},{25,17},{10,2},{18,10},{26,18},{... | collective-permute-start | bytes 393224 | tf_op jit(solution)/shard_map/ppermute | solution.py:17
  149.9 2.4 %collective-permute-start.1 = (f32[1,64,512]{2,0,1:T(1,128)S(1)}, f32[1,64,512]{2,0,1:T(1,128)S(1)}, u32[]{:S(2)}, u32[]{:S(2)}) collective-permute-start(f32[1,64,512]{2,0,1:T(1,128)S(1)} %get-tuple-element.7), channel_id=1, source_target_pairs={{0,8},{8,16},{16,24},{1,9},{9,17},{17,25},{2,10},{10,18},{18,26},{... | collective-permute-start | bytes 393224 | tf_op jit(solution)/shard_map/ppermute | solution.py:15
  152.3 0.1 collective-permute-done
  152.4 3.8 %collective-permute-done.1 = f32[1,64,512]{2,0,1:T(1,128)S(1)} collective-permute-done((f32[1,64,512]{2,0,1:T(1,128)S(1)}, f32[1,64,512]{2,0,1:T(1,128)S(1)}, u32[]{:S(2)}, u32[]{:S(2)}) %collective-permute-start.1) | collective-permute-done | bytes 131104 | tf_op jit(solution)/shard_map/ppermute | solution.py:15
  156.2 3.4 %collective-permute-start.2 = (f32[4,1,512]{2,0,1:T(4,128)S(1)}, f32[4,1,512]{2,0,1:T(4,128)S(1)}, u32[]{:S(2)}, u32[]{:S(2)}) collective-permute-start(f32[4,1,512]{2,0,1:T(4,128)S(1)} %get-tuple-element.6), channel_id=1, source_target_pairs={{1,0},{2,1},{3,2},{4,3},{5,4},{6,5},{7,6},{9,8},{10,9},{11,10},{12... | collective-permute-start | bytes 24584 | tf_op jit(solution)/shard_map/ppermute | solution.py:17
  159.6 2.5 %collective-permute-start.3 = (f32[4,1,512]{2,0,1:T(4,128)S(1)}, f32[4,1,512]{2,0,1:T(4,128)S(1)}, u32[]{:S(2)}, u32[]{:S(2)}) collective-permute-start(f32[4,1,512]{2,0,1:T(4,128)S(1)} %get-tuple-element.5), channel_id=1, source_target_pairs={{0,1},{1,2},{2,3},{3,4},{4,5},{5,6},{6,7},{8,9},{9,10},{10,11},{11... | collective-permute-start | bytes 24584 | tf_op jit(solution)/shard_map/ppermute | solution.py:15
  162.1 0.0 collective-permute-done.2
  162.1 3.9 %collective-permute-done.3 = f32[4,1,512]{2,0,1:T(4,128)S(1)} collective-permute-done((f32[4,1,512]{2,0,1:T(4,128)S(1)}, f32[4,1,512]{2,0,1:T(4,128)S(1)}, u32[]{:S(2)}, u32[]{:S(2)}) %collective-permute-start.3) | collective-permute-done | bytes 8224 | tf_op jit(solution)/shard_map/ppermute | solution.py:15
  166.0 1.1 select_maximum_fusion
  167.2 2.5 %fusion.1 = f32[2,64,512]{2,0,1:T(2,128)S(1)} fusion(f32[4,66,514]{2,0,1:T(4,128)S(1)} %select_maximum_fusion, f32[4,1,512]{2,0,1:T(4,128)S(1)} %collective-permute-done.3, f32[1,64,512]{2,0,1:T(1,128)S(1)} %collective-permute-done, f32[2,64,512]{2,0,1:T(2,128)S(1)} %dynamic-slice_multiply_fusion, f32[1,64,512]{2,0,1:T(1,128)S(1)} %collective-permute-done.1, ...), kind=kLoop, calls=%fused_computation.9 | loop fusion | flops 983040 | bytes 1589252 | tf_op jit(solution)/shard_map/sub | solution.py:40
  169.6 0.8 copy.4
  (1 shorter events, 0.0 us)
Async XLA Ops:
  6.5 139.9 %all-reduce.3.cloned.1.call-start = ((), (), s32[]{:S(2)}) async-start(), calls=%async_computation.1 | async-start | bytes 2097152 | tf_op jit(solution)/shard_map/psum | solution.py:31
  148.0 4.4 %collective-permute-start = (f32[1,64,512]{2,0,1:T(1,128)S(1)}, f32[1,64,512]{2,0,1:T(1,128)S(1)}, u32[]{:S(2)}, u32[]{:S(2)}) collective-permute-start(f32[1,64,512]{2,0,1:T(1,128)S(1)} %get-tuple-element.8), channel_id=1, source_target_pairs={{8,0},{16,8},{24,16},{9,1},{17,9},{25,17},{10,2},{18,10},{26,18},{... | collective-permute-start | bytes 393224 | tf_op jit(solution)/shard_map/ppermute | solution.py:17
  149.9 6.3 %collective-permute-start.1 = (f32[1,64,512]{2,0,1:T(1,128)S(1)}, f32[1,64,512]{2,0,1:T(1,128)S(1)}, u32[]{:S(2)}, u32[]{:S(2)}) collective-permute-start(f32[1,64,512]{2,0,1:T(1,128)S(1)} %get-tuple-element.7), channel_id=1, source_target_pairs={{0,8},{8,16},{16,24},{1,9},{9,17},{17,25},{2,10},{10,18},{18,26},{... | collective-permute-start | bytes 393224 | tf_op jit(solution)/shard_map/ppermute | solution.py:15
  156.2 5.9 %collective-permute-start.2 = (f32[4,1,512]{2,0,1:T(4,128)S(1)}, f32[4,1,512]{2,0,1:T(4,128)S(1)}, u32[]{:S(2)}, u32[]{:S(2)}) collective-permute-start(f32[4,1,512]{2,0,1:T(4,128)S(1)} %get-tuple-element.6), channel_id=1, source_target_pairs={{1,0},{2,1},{3,2},{4,3},{5,4},{6,5},{7,6},{9,8},{10,9},{11,10},{12... | collective-permute-start | bytes 24584 | tf_op jit(solution)/shard_map/ppermute | solution.py:17
  159.6 6.4 %collective-permute-start.3 = (f32[4,1,512]{2,0,1:T(4,128)S(1)}, f32[4,1,512]{2,0,1:T(4,128)S(1)}, u32[]{:S(2)}, u32[]{:S(2)}) collective-permute-start(f32[4,1,512]{2,0,1:T(4,128)S(1)} %get-tuple-element.5), channel_id=1, source_target_pairs={{0,1},{1,2},{2,3},{3,4},{4,5},{5,6},{6,7},{8,9},{9,10},{10,11},{11... | collective-permute-start | bytes 24584 | tf_op jit(solution)/shard_map/ppermute | solution.py:15
Sparse Core Ops, SparseCore 0:
  111.1 35.2 all-reduce.2
where the time goes:
time: 178 us; the launch traced here: 177 us
  blocking collectives  98.3 us (55%)
  waiting for transfers between devices  43.2 us (24%)
  between operations  13.5 us (8%)
  starting transfers between devices  10.2 us (6%)
  other arithmetic  6.56 us (4%)
  local copies, waits for them, and re-layouts  5.48 us (3%)
    all_to_all x1, blocking collectives, body(): lax.all_to_all(partials, 'tile', split_axis=2, concat_axis=0, tiled=True)  98.3 us
    psum x1, waiting for transfers between devices, body(): full = lax.psum(strip, 'shot')  35.4 us
    ppermute x2, waiting for transfers between devices, padded_2(): lax.ppermute(tail, axis, [(i, (i + 1) % count) for i in range(ends)])  7.73 us
    ppermute x2, starting transfers between devices, padded_2(): lax.ppermute(head, axis, [((i + 1) % count, i) for i in range(ends)])  5.28 us
    ppermute x2, starting transfers between devices, padded_2(): lax.ppermute(tail, axis, [(i, (i + 1) % count) for i in range(ends)])  4.89 us
    unnamed x1, local copies, waits for them, and re-layouts  4.53 us
  transfers between devices with their start and end apart: 5, of which 4 were waited for; matrix products, arithmetic and copies ran while one was open for 0% of the time, Pallas kernels for 0%

commit v1 on v0

v1 whole, which is shorter than its diff:
```python
import functools

import jax
import jax.numpy as jnp
from jax import lax
from jax.experimental import pallas as pl
from jax.experimental.pallas import tpu as pltpu
from jax.sharding import PartitionSpec as P

MESH = pl.DeviceIdType.MESH
F32 = jnp.float32


def kernel(groups, members, src, out, own_a, own_b, r1a, r1b, s1a, s1b, r2a, r2b,
           s2, r3, s3, r4, img, low, high, top, bottom, own_sem,
           p1s, p1r, q1s, q1r, p2s, p2r, p3s, p3r, hs, hr):
    nd, nz, rows, width = src.shape[2], src.shape[3], src.shape[5], src.shape[6]
    cw = width // 4
    edge = top.shape[1]
    steps = 2 * nd
    g, t = lax.axis_index("shot"), lax.axis_index("tile")
    x, c = g // 2, g % 2
    z, y = t // 2, t % 2

    def dev(gx, tx):
        return {"shot": gx, "tile": tx}

    x_peer = dev((1 - x) * 2 + c, t)
    c_peer = dev(x * 2 + 1 - c, t)
    y_peer = dev(g, z * 2 + 1 - y)

    def z_peer(o):
        return dev(g, lax.rem(z + o, nz) * 2 + y)

    beside = [
        (g > 0, dev(g - 1, t)),
        (g < groups - 1, dev(g + 1, t)),
        (t > 0, dev(g, t - 1)),
        (t < members - 1, dev(g, t + 1)),
    ]

    loads = [
        pltpu.make_async_copy(src.at[x, :, :, :, :, :, pl.ds(0, 2 * cw)], own_a, own_sem.at[0]),
        pltpu.make_async_copy(src.at[:, :, :, :, y, :, pl.ds(2 * cw, 2 * cw)], own_b, own_sem.at[1]),
    ]
    for copy in loads:
        copy.start()

    barrier = pltpu.get_barrier_semaphore()
    peers = [x_peer, c_peer, y_peer] + [z_peer(o) for o in range(1, nz)]
    count = jnp.int32(len(peers))
    for peer in peers:
        pl.semaphore_signal(barrier, inc=1, device_id=peer, device_id_type=MESH)
    for there, peer in beside:
        count = count + jnp.where(there, 1, 0)

        @pl.when(there)
        def _():
            pl.semaphore_signal(barrier, inc=1, device_id=peer, device_id_type=MESH)
    pl.semaphore_wait(barrier, count)

    sends = []

    def remote(a, b, s, r, peer):
        copy = pltpu.make_async_remote_copy(
            src_ref=a, dst_ref=b, send_sem=s, recv_sem=r, device_id=peer, device_id_type=MESH
        )
        copy.start()
        sends.append(copy)
        return copy

    first, second, third, fourth = {}, {}, {}, {}

    def p1(k):
        block, d = k // nd, k % nd
        first[k] = (
            remote(src.at[1 - x, :, d, :, :, :, pl.ds(block * cw, cw)], r1a.at[k],
                   p1s.at[0, k], p1r.at[0, k], x_peer),
            remote(src.at[:, :, d, :, 1 - y, :, pl.ds((2 + block) * cw, cw)], r1b.at[k],
                   p1s.at[1, k], p1r.at[1, k], y_peer),
        )

    def two_a(k, core, side):
        block, d = k // nd, k % nd
        own = own_a[core, d, :, side, :, pl.ds(block * cw, cw)]
        return own.astype(F32) + r1a[k, core, :, side].astype(F32)

    def two_b(k, core, side):
        block, d = k // nd, k % nd
        own = own_b[side, core, d, :, :, pl.ds(block * cw, cw)]
        return own.astype(F32) + r1b[k, side, core].astype(F32)

    def q1(k):
        a, b = first[k]
        a.wait_recv()
        for side in range(2):
            s1a[k, side] = two_a(k, 1 - c, side)
        ca = remote(s1a.at[k], r2a.at[k], q1s.at[0, k], q1r.at[0, k], c_peer)
        b.wait_recv()
        for side in range(2):
            s1b[k, side] = two_b(k, 1 - c, side)
        cb = remote(s1b.at[k], r2b.at[k], q1s.at[1, k], q1r.at[1, k], c_peer)
        second[k] = (ca, cb)

    def p2(k):
        a, b = second[k]
        a.wait_recv()
        s2[0, k] = two_a(k, c, 1 - y) + r2a[k, 1 - y]
        ca = remote(s2.at[0, k], r3.at[0, k], p2s.at[0, k], p2r.at[0, k], y_peer)
        b.wait_recv()
        s2[1, k] = two_b(k, c, 1 - x) + r2b[k, 1 - x]
        cb = remote(s2.at[1, k], r3.at[1, k], p2s.at[1, k], p2r.at[1, k], x_peer)
        third[k] = (ca, cb)

    def p3(k):
        copies = []
        for kind in range(2):
            third[k][kind].wait_recv()
            if kind == 0:
                s3[0, k] = two_a(k, c, y) + r2a[k, y] + r3[0, k]
            else:
                s3[1, k] = two_b(k, c, x) + r2b[k, x] + r3[1, k]
            for o in range(1, nz):
                to = lax.rem(z + o, nz)
                copies.append(remote(s3.at[kind, k, to], r4.at[kind, k, z],
                                     p3s.at[kind, k, o - 1], p3r.at[kind, k, o - 1], z_peer(o)))
        fourth[k] = copies

    scale = 1.0 / jnp.sqrt(F32(groups * members))
    halo_waits = []

    def halo(there_to, peer_to, there_from, peer_from, a, b, s, r):
        def make(peer):
            return pltpu.make_async_remote_copy(
                src_ref=a, dst_ref=b, send_sem=s, recv_sem=r, device_id=peer, device_id_type=MESH
            )

        @pl.when(there_to)
        def _():
            make(peer_to).start()

        def done():
            @pl.when(there_from)
            def _():
                make(peer_from).wait_recv()

            @pl.when(there_to)
            def _():
                make(peer_to).wait_send()

        halo_waits.append(done)

    def last(k):
        block, d = k // nd, k % nd
        for kind in range(2):
            cols = pl.ds((2 * kind + block) * cw, cw)
            total = s3[kind, k, z]
            for o in range(1, nz):
                fourth[k][kind * (nz - 1) + o - 1].wait_recv()
                total = total + r4[kind, k, lax.rem(z + nz - o, nz)]
            img[d, :, cols] = total * scale
            if d == 0:
                halo(*beside[0], *beside[1], img.at[d, :, cols], high.at[:, cols], hs.at[0, kind, k], hr.at[0, kind, k])
            if d == nd - 1:
                halo(*beside[1], *beside[0], img.at[d, :, cols], low.at[:, cols], hs.at[1, kind, k], hr.at[1, kind, k])
            halo(*beside[2], *beside[3], img.at[d, pl.ds(0, edge), cols], bottom.at[d, :, cols],
                 hs.at[2, kind, k], hr.at[2, kind, k])
            halo(*beside[3], *beside[2], img.at[d, pl.ds(rows - edge, edge), cols], top.at[d, :, cols],
                 hs.at[3, kind, k], hr.at[3, kind, k])

    p1(0)
    p1(1)
    for copy in loads:
        copy.wait()
    for k in range(steps):
        q1(k)
        p2(k)
        if k + 2 < steps:
            p1(k + 2)
        if k >= 1:
            p3(k - 1)
        if k >= 2:
            last(k - 2)
    last(steps - 2)
    p3(steps - 1)
    last(steps - 1)
    for done in halo_waits:
        done()

    row = lax.broadcasted_iota(jnp.int32, (rows, width), 0)
    col = lax.broadcasted_iota(jnp.int32, (rows, width), 1)
    for d in range(nd):
        here = img[d]
        below = img[d - 1] if d > 0 else jnp.where(g > 0, low[...], 0.0)
        above = img[d + 1] if d < nd - 1 else jnp.where(g < groups - 1, high[...], 0.0)
        before = jnp.where(t > 0, top[d, edge - 1:edge, :], 0.0)
        after = jnp.where(t < members - 1, bottom[d, 0:1, :], 0.0)
        near = above + below
        near = near + jnp.where(row == rows - 1, after, pltpu.roll(here, rows - 1, 0))
        near = near + jnp.where(row == 0, before, pltpu.roll(here, 1, 0))
        near = near + jnp.where(col == width - 1, 0.0, pltpu.roll(here, width - 1, 1))
        near = near + jnp.where(col == 0, 0.0, pltpu.roll(here, 1, 1))
        out[d] = 6.0 * here - near
    for copy in sends:
        copy.wait_send()


def body(groups, members, partials):
    shots, depth, lateral, width = partials.shape
    nd, nz, rows, cw = depth // groups, members // 2, lateral // members, width // 4
    steps, edge = 2 * nd, min(8, rows)
    src = partials.reshape(2, 2, nd, nz, 2, rows, width)
    kind = partials.dtype
    dma = pltpu.SemaphoreType.DMA
    return pl.pallas_call(
        functools.partial(kernel, groups, members),
        out_shape=jax.ShapeDtypeStruct((nd, rows, width), F32),
        in_specs=[pl.BlockSpec(memory_space=pl.ANY)],
        out_specs=pl.BlockSpec(memory_space=pltpu.VMEM),
        scratch_shapes=[
            pltpu.VMEM((2, nd, nz, 2, rows, 2 * cw), kind),
            pltpu.VMEM((2, 2, nd, nz, rows, 2 * cw), kind),
            pltpu.VMEM((steps, 2, nz, 2, rows, cw), kind),
            pltpu.VMEM((steps, 2, 2, nz, rows, cw), kind),
            pltpu.VMEM((steps, 2, nz, rows, cw), F32),
            pltpu.VMEM((steps, 2, nz, rows, cw), F32),
            pltpu.VMEM((steps, 2, nz, rows, cw), F32),
            pltpu.VMEM((steps, 2, nz, rows, cw), F32),
            pltpu.VMEM((2, steps, nz, rows, cw), F32),
            pltpu.VMEM((2, steps, nz, rows, cw), F32),
            pltpu.VMEM((2, steps, nz, rows, cw), F32),
            pltpu.VMEM((2, steps, nz, rows, cw), F32),
            pltpu.VMEM((nd, rows, width), F32),
            pltpu.VMEM((rows, width), F32),
            pltpu.VMEM((rows, width), F32),
            pltpu.VMEM((nd, edge, width), F32),
            pltpu.VMEM((nd, edge, width), F32),
            dma((2,)),
            dma((2, steps)), dma((2, steps)),
            dma((2, steps)), dma((2, steps)),
            dma((2, steps)), dma((2, steps)),
            dma((2, steps, nz - 1)), dma((2, steps, nz - 1)),
            dma((4, 2, steps)), dma((4, 2, steps)),
        ],
        compiler_params=pltpu.CompilerParams(collective_id=0, has_side_effects=True),
    )(src)


def solution(mesh):
    groups, members = mesh.shape["shot"], mesh.shape["tile"]
    return jax.shard_map(
        functools.partial(body, groups, members),
        mesh=mesh,
        in_specs=(P(("shot", "tile"), None, None, None),),
        out_specs=P("shot", "tile", None),
        check_vma=False,
    )
```

time: 178 us -> 58.9 us (0.33)
  the two profiles are of different devices: /device:TPU:10 before, /device:TPU:0 now
where the time goes in v1:
time: 58.9 us; the launch traced here: 58.8 us
  Pallas kernels  57.1 us (97%)
  local copies, waits for them, and re-layouts  1.67 us (3%)
    pallas_call x1, Pallas kernels, body(): pl.pallas_call(functools.partial(kernel, groups, members), out_shape=jax....  57.1 us
    unnamed x1, local copies, waits for them, and re-layouts  1.67 us

profile of v1, /device:TPU:0, one launch (start us, length us, event | category | flops | bytes accessed | tf_op | source)
XLA Modules:
  0.0 58.8 jit_solution(10106909636052626192)
XLA Ops:
  0.0 57.1 %shard_map.17 = f32[2,64,512]{2,1,0:T(8,128)} custom-call(bf16[2,2,2,4,2,64,512]{6,5,4,3,2,1,0:T(8,128)(2,1)} %bitcast.1), custom_call_target="tpu_custom_call" | custom-call | tf_op jit(solution)/shard_map/pallas_call | solution.py:215
  57.1 1.7 %copy.3 = f32[2,64,512]{2,1,0:T(8,128)} copy(f32[2,64,512]{2,1,0:T(8,128)} %shard_map.17) | data formatting | bytes 524288

commit v2 on v1

v2 whole, which is shorter than its diff:
```python
import functools

import jax
import jax.numpy as jnp
from jax import lax
from jax.experimental import pallas as pl
from jax.experimental.pallas import tpu as pltpu
from jax.sharding import PartitionSpec as P

MESH = pl.DeviceIdType.MESH
F32 = jnp.float32


def kernel(groups, members, src, out, own_a, own_b, own_c, r1a, r1b, s1a, s1b, r2a, r2b,
           s2, r3, s3, r4, rz, sc, rc, tc, rd, img, low, high, top, bottom, own_sem,
           p1s, p1r, q1s, q1r, p2s, p2r, p3s, p3r, zs, zr, cs, cr, ds, dr, hs, hr):
    nd, nz, rows, width = src.shape[2], src.shape[3], src.shape[5], src.shape[6]
    cw = width // 4
    rr = s2.shape[3]
    parts = rows // rr
    edge = top.shape[1]
    units = [(j, d, h) for j in range(2) for d in range(nd) for h in range(parts)]
    cj, cd, ch = units.pop()
    steps = len(units)
    g, t = lax.axis_index("shot"), lax.axis_index("tile")
    x, c = g // 2, g % 2
    z, y = t // 2, t % 2

    def dev(gx, tx):
        return {"shot": gx, "tile": tx}

    x_peer = dev((1 - x) * 2 + c, t)
    c_peer = dev(x * 2 + 1 - c, t)
    y_peer = dev(g, z * 2 + 1 - y)
    d_peer = dev((1 - x) * 2 + c, z * 2 + 1 - y)

    def z_peer(o):
        return dev(g, lax.rem(z + o, nz) * 2 + y)

    beside = [
        (g > 0, dev(g - 1, t)),
        (g < groups - 1, dev(g + 1, t)),
        (t > 0, dev(g, t - 1)),
        (t < members - 1, dev(g, t + 1)),
    ]

    def col(kind, j):
        return pl.ds((2 * kind + j) * cw, cw)

    def row(h):
        return pl.ds(h * rr, rr)

    barrier = pltpu.get_barrier_semaphore()
    peers = [x_peer, c_peer, y_peer, d_peer] + [z_peer(o) for o in range(1, nz)]
    count = jnp.int32(len(peers))
    for peer in peers:
        pl.semaphore_signal(barrier, inc=1, device_id=peer, device_id_type=MESH)
    for there, peer in beside:
        count = count + jnp.where(there, 1, 0)

        @pl.when(there)
        def _():
            pl.semaphore_signal(barrier, inc=1, device_id=peer, device_id_type=MESH)
    loads = [
        pltpu.make_async_copy(src.at[x, :, :, :, :, :, pl.ds(0, 2 * cw)], own_a, own_sem.at[0]),
        pltpu.make_async_copy(src.at[:, :, :, :, y, :, pl.ds(2 * cw, 2 * cw)], own_b, own_sem.at[1]),
    ]
    for kind in range(2):
        loads.append(pltpu.make_async_copy(src.at[:, :, cd, z, :, row(ch), col(kind, cj)],
                                           own_c.at[kind], own_sem.at[2 + kind]))
    for copy in loads:
        copy.start()
    pl.semaphore_wait(barrier, count)

    sends = []

    def remote(a, b, s, r, peer):
        copy = pltpu.make_async_remote_copy(
            src_ref=a, dst_ref=b, send_sem=s, recv_sem=r, device_id=peer, device_id_type=MESH
        )
        copy.start()
        sends.append(copy)
        return copy

    first, second, third, fourth = {}, {}, {}, {}

    def p1(k):
        j, d, h = units[k]
        first[k] = (
            remote(src.at[1 - x, :, d, :, :, row(h), col(0, j)], r1a.at[k],
                   p1s.at[0, k], p1r.at[0, k], x_peer),
            remote(src.at[:, :, d, :, 1 - y, row(h), col(1, j)], r1b.at[k],
                   p1s.at[1, k], p1r.at[1, k], y_peer),
        )

    def two_a(k, core, side):
        j, d, h = units[k]
        own = own_a[core, d, :, side, row(h), pl.ds(j * cw, cw)]
        return own.astype(F32) + r1a[k, core, :, side].astype(F32)

    def two_b(k, core, side):
        j, d, h = units[k]
        own = own_b[side, core, d, :, row(h), pl.ds(j * cw, cw)]
        return own.astype(F32) + r1b[k, side, core].astype(F32)

    def q1(k):
        a, b = first[k]
        a.wait_recv()
        for side in range(2):
            s1a[k, side] = two_a(k, 1 - c, side)
        ca = remote(s1a.at[k], r2a.at[k], q1s.at[0, k], q1r.at[0, k], c_peer)
        b.wait_recv()
        for side in range(2):
            s1b[k, side] = two_b(k, 1 - c, side)
        cb = remote(s1b.at[k], r2b.at[k], q1s.at[1, k], q1r.at[1, k], c_peer)
        second[k] = (ca, cb)

    def p2(k):
        a, b = second[k]
        a.wait_recv()
        s2[0, k] = two_a(k, c, 1 - y) + r2a[k, 1 - y]
        ca = remote(s2.at[0, k], r3.at[0, k], p2s.at[0, k], p2r.at[0, k], y_peer)
        b.wait_recv()
        s2[1, k] = two_b(k, c, 1 - x) + r2b[k, 1 - x]
        cb = remote(s2.at[1, k], r3.at[1, k], p2s.at[1, k], p2r.at[1, k], x_peer)
        third[k] = (ca, cb)

    def p3(k):
        copies = []
        for kind in range(2):
            third[k][kind].wait_recv()
            if kind == 0:
                s3[0, k] = two_a(k, c, y) + r2a[k, y] + r3[0, k]
            else:
                s3[1, k] = two_b(k, c, x) + r2b[k, x] + r3[1, k]
            for o in range(1, nz):
                to = lax.rem(z + o, nz)
                copies.append(remote(s3.at[kind, k, to], r4.at[kind, k, z],
                                     p3s.at[kind, k, o - 1], p3r.at[kind, k, o - 1], z_peer(o)))
        fourth[k] = copies

    z_first, z_core, z_last = [], [], []

    def c_z():
        for kind in range(2):
            for o in range(1, nz):
                to = lax.rem(z + o, nz)
                z_first.append(remote(src.at[:, :, cd, to, :, row(ch), col(kind, cj)], rz.at[kind, o - 1],
                                      zs.at[kind, o - 1], zr.at[kind, o - 1], z_peer(o)))

    def c_sum(kind, core, side):
        total = own_c[kind, side, core].astype(F32)
        for o in range(1, nz):
            total = total + rz[kind, o - 1, side, core].astype(F32)
        return total

    def c_core():
        for kind in range(2):
            for o in range(1, nz):
                z_first[kind * (nz - 1) + o - 1].wait_recv()
            for side in range(2):
                sc[kind, side] = c_sum(kind, 1 - c, side)
            z_core.append(remote(sc.at[kind], rc.at[kind], cs.at[kind], cr.at[kind], c_peer))

    def c_xy():
        for kind in range(2):
            z_core[kind].wait_recv()
            for side in range(2):
                tc[kind, side] = c_sum(kind, c, side) + rc[kind, side]
            for i, (a, b, peer) in enumerate(
                [(1 - x, 1 - y, d_peer), (1 - x, y, x_peer), (x, 1 - y, y_peer)]
            ):
                z_last.append(remote(tc.at[kind, a, b], rd.at[kind, i], ds.at[kind, i], dr.at[kind, i], peer))

    scale = 1.0 / jnp.sqrt(F32(groups * members))
    halo_waits = []

    def halo(there_to, peer_to, there_from, peer_from, a, b, s, r):
        def make(peer):
            return pltpu.make_async_remote_copy(
                src_ref=a, dst_ref=b, send_sem=s, recv_sem=r, device_id=peer, device_id_type=MESH
            )

        @pl.when(there_to)
        def _():
            make(peer_to).start()

        def done():
            @pl.when(there_from)
            def _():
                make(peer_from).wait_recv()

            @pl.when(there_to)
            def _():
                make(peer_to).wait_send()

        halo_waits.append(done)

    def finish(kind, unit, k, total):
        j, d, h = unit
        cols = col(kind, j)
        img[d, row(h), cols] = total * scale
        if d == 0:
            halo(*beside[0], *beside[1], img.at[d, row(h), cols], high.at[row(h), cols],
                 hs.at[0, kind, k], hr.at[0, kind, k])
        if d == nd - 1:
            halo(*beside[1], *beside[0], img.at[d, row(h), cols], low.at[row(h), cols],
                 hs.at[1, kind, k], hr.at[1, kind, k])
        if h == 0:
            halo(*beside[2], *beside[3], img.at[d, pl.ds(0, edge), cols], bottom.at[d, :, cols],
                 hs.at[2, kind, k], hr.at[2, kind, k])
        if h == parts - 1:
            halo(*beside[3], *beside[2], img.at[d, pl.ds(rows - edge, edge), cols], top.at[d, :, cols],
                 hs.at[3, kind, k], hr.at[3, kind, k])

    def last(k):
        for kind in range(2):
            total = s3[kind, k, z]
            for o in range(1, nz):
                fourth[k][kind * (nz - 1) + o - 1].wait_recv()
                total = total + r4[kind, k, lax.rem(z + nz - o, nz)]
            finish(kind, units[k], k, total)

    def c_last():
        for kind in range(2):
            total = tc[kind, x, y]
            for i in range(3):
                z_last[kind * 3 + i].wait_recv()
                total = total + rd[kind, i]
            finish(kind, (cj, cd, ch), steps, total)

    at_core = min(3, steps - 1)
    at_xy = max(steps - 2, at_core)
    ahead = 3
    p1(0)
    c_z()
    for k in range(1, min(ahead, steps)):
        p1(k)
    for copy in loads:
        copy.wait()
    for k in range(steps):
        q1(k)
        p2(k)
        if k + ahead < steps:
            p1(k + ahead)
        if k >= 2:
            p3(k - 2)
        if k == at_core:
            c_core()
        if k == at_xy:
            c_xy()
        if k >= 4:
            last(k - 4)
    for k in range(max(steps - 2, 0), steps):
        p3(k)
    for k in range(max(steps - 4, 0), steps - 1):
        last(k)
    c_last()
    last(steps - 1)
    for done in halo_waits:
        done()

    rown = lax.broadcasted_iota(jnp.int32, (rows, width), 0)
    coln = lax.broadcasted_iota(jnp.int32, (rows, width), 1)
    for d in range(nd):
        here = img[d]
        below = img[d - 1] if d > 0 else jnp.where(g > 0, low[...], 0.0)
        above = img[d + 1] if d < nd - 1 else jnp.where(g < groups - 1, high[...], 0.0)
        before = jnp.where(t > 0, top[d, edge - 1:edge, :], 0.0)
        after = jnp.where(t < members - 1, bottom[d, 0:1, :], 0.0)
        near = above + below
        near = near + jnp.where(rown == rows - 1, after, pltpu.roll(here, rows - 1, 0))
        near = near + jnp.where(rown == 0, before, pltpu.roll(here, 1, 0))
        near = near + jnp.where(coln == width - 1, 0.0, pltpu.roll(here, width - 1, 1))
        near = near + jnp.where(coln == 0, 0.0, pltpu.roll(here, 1, 1))
        out[d] = 6.0 * here - near
    for copy in sends:
        copy.wait_send()


def body(groups, members, partials):
    shots, depth, lateral, width = partials.shape
    nd, nz, rows, cw = depth // groups, members // 2, lateral // members, width // 4
    parts = 2 if rows % 32 == 0 else 1
    rr, edge = rows // parts, min(8, rows)
    steps = 2 * nd * parts - 1
    src = partials.reshape(2, 2, nd, nz, 2, rows, width)
    kind = partials.dtype
    dma = pltpu.SemaphoreType.DMA
    return pl.pallas_call(
        functools.partial(kernel, groups, members),
        out_shape=jax.ShapeDtypeStruct((nd, rows, width), F32),
        in_specs=[pl.BlockSpec(memory_space=pl.ANY)],
        out_specs=pl.BlockSpec(memory_space=pltpu.VMEM),
        scratch_shapes=[
            pltpu.VMEM((2, nd, nz, 2, rows, 2 * cw), kind),
            pltpu.VMEM((2, 2, nd, nz, rows, 2 * cw), kind),
            pltpu.VMEM((2, 2, 2, 2, rr, cw), kind),
            pltpu.VMEM((steps, 2, nz, 2, rr, cw), kind),
            pltpu.VMEM((steps, 2, 2, nz, rr, cw), kind),
            pltpu.VMEM((steps, 2, nz, rr, cw), F32),
            pltpu.VMEM((steps, 2, nz, rr, cw), F32),
            pltpu.VMEM((steps, 2, nz, rr, cw), F32),
            pltpu.VMEM((steps, 2, nz, rr, cw), F32),
            pltpu.VMEM((2, steps, nz, rr, cw), F32),
            pltpu.VMEM((2, steps, nz, rr, cw), F32),
            pltpu.VMEM((2, steps, nz, rr, cw), F32),
            pltpu.VMEM((2, steps, nz, rr, cw), F32),
            pltpu.VMEM((2, nz - 1, 2, 2, 2, rr, cw), kind),
            pltpu.VMEM((2, 2, 2, rr, cw), F32),
            pltpu.VMEM((2, 2, 2, rr, cw), F32),
            pltpu.VMEM((2, 2, 2, rr, cw), F32),
            pltpu.VMEM((2, 3, rr, cw), F32),
            pltpu.VMEM((nd, rows, width), F32),
            pltpu.VMEM((rows, width), F32),
            pltpu.VMEM((rows, width), F32),
            pltpu.VMEM((nd, edge, width), F32),
            pltpu.VMEM((nd, edge, width), F32),
            dma((4,)),
            dma((2, steps)), dma((2, steps)),
            dma((2, steps)), dma((2, steps)),
            dma((2, steps)), dma((2, steps)),
            dma((2, steps, nz - 1)), dma((2, steps, nz - 1)),
            dma((2, nz - 1)), dma((2, nz - 1)),
            dma((2,)), dma((2,)),
            dma((2, 3)), dma((2, 3)),
            dma((4, 2, steps + 1)), dma((4, 2, steps + 1)),
        ],
        compiler_params=pltpu.CompilerParams(collective_id=0, has_side_effects=True),
    )(src)


def solution(mesh):
    groups, members = mesh.shape["shot"], mesh.shape["tile"]
    return jax.shard_map(
        functools.partial(body, groups, members),
        mesh=mesh,
        in_specs=(P(("shot", "tile"), None, None, None),),
        out_specs=P("shot", "tile", None),
        check_vma=False,
    )
```

time: 58.9 us -> 53.8 us (0.913)
  Pallas kernels: 57.1 us -> 51.9 us
    pallas_call x1, Pallas kernels: 57.1 us -> 51.9 us  [body(): pl.pallas_call(functools.partial(kernel, groups, members), out_shape=jax....]
where the time goes in v2:
time: 53.8 us; the launch traced here: 53.6 us
  Pallas kernels  51.9 us (96%)
  local copies, waits for them, and re-layouts  1.67 us (3%)
    pallas_call x1, Pallas kernels, body(): pl.pallas_call(functools.partial(kernel, groups, members), out_shape=jax....  51.9 us
    unnamed x1, local copies, waits for them, and re-layouts  1.67 us

profile of v2, /device:TPU:0, one launch (start us, length us, event | category | flops | bytes accessed | tf_op | source)
XLA Modules:
  0.0 53.6 jit_solution(12051507653899592813)
XLA Ops:
  0.0 51.9 %shard_map.17 = f32[2,64,512]{2,1,0:T(8,128)} custom-call(bf16[2,2,2,4,2,64,512]{6,5,4,3,2,1,0:T(8,128)(2,1)} %bitcast.1), custom_call_target="tpu_custom_call" | custom-call | tf_op jit(solution)/shard_map/pallas_call | solution.py:290
  51.9 1.7 %copy.3 = f32[2,64,512]{2,1,0:T(8,128)} copy(f32[2,64,512]{2,1,0:T(8,128)} %shard_map.17) | data formatting | bytes 524288

commit v3 on v2

v3 whole, which is shorter than its diff:
```python
import functools

import jax
import jax.numpy as jnp
from jax import lax
from jax.experimental import pallas as pl
from jax.experimental.pallas import tpu as pltpu
from jax.sharding import PartitionSpec as P

MESH = pl.DeviceIdType.MESH
F32 = jnp.float32


def kernel(groups, members, src, out, own_a, own_b, own_c, r1a, r1b, s1a, s1b, r2a, r2b,
           s2, r3, s3, r4, rz, sc, rc, tc, rd, img, low, high, top, bottom, own_sem,
           p1s, p1r, q1s, q1r, p2s, p2r, p3s, p3r, zs, zr, cs, cr, ds, dr, hs, hr):
    nd, nz, rows, width = src.shape[2], src.shape[3], src.shape[5], src.shape[6]
    cw = width // 4
    rr = s2.shape[3]
    parts = rows // rr
    edge = top.shape[1]
    units = [(j, d, h * rr) for j in range(2) for d in range(nd) for h in range(parts)]
    crows = own_c.shape[4]
    c_unit = (1, nd - 1, rows - crows)
    cj, cd, ch = c_unit
    units = units[: len(units) - crows // rr]
    steps = len(units)
    g, t = lax.axis_index("shot"), lax.axis_index("tile")
    x, c = g // 2, g % 2
    z, y = t // 2, t % 2

    def dev(gx, tx):
        return {"shot": gx, "tile": tx}

    x_peer = dev((1 - x) * 2 + c, t)
    c_peer = dev(x * 2 + 1 - c, t)
    y_peer = dev(g, z * 2 + 1 - y)
    d_peer = dev((1 - x) * 2 + c, z * 2 + 1 - y)

    def z_peer(o):
        return dev(g, lax.rem(z + o, nz) * 2 + y)

    beside = [
        (g > 0, dev(g - 1, t)),
        (g < groups - 1, dev(g + 1, t)),
        (t > 0, dev(g, t - 1)),
        (t < members - 1, dev(g, t + 1)),
    ]

    def col(kind, j):
        return pl.ds((2 * kind + j) * cw, cw)

    def row(h):
        return pl.ds(h, rr)

    c_row = pl.ds(ch, crows)

    barrier = pltpu.get_barrier_semaphore()
    peers = [x_peer, c_peer, y_peer, d_peer] + [z_peer(o) for o in range(1, nz)]
    count = jnp.int32(len(peers))
    for peer in peers:
        pl.semaphore_signal(barrier, inc=1, device_id=peer, device_id_type=MESH)
    for there, peer in beside:
        count = count + jnp.where(there, 1, 0)

        @pl.when(there)
        def _():
            pl.semaphore_signal(barrier, inc=1, device_id=peer, device_id_type=MESH)
    loads = [
        pltpu.make_async_copy(src.at[x, :, :, :, :, :, pl.ds(0, 2 * cw)], own_a, own_sem.at[0]),
        pltpu.make_async_copy(src.at[:, :, :, :, y, :, pl.ds(2 * cw, 2 * cw)], own_b, own_sem.at[1]),
    ]
    for kind in range(2):
        loads.append(pltpu.make_async_copy(src.at[:, :, cd, z, :, c_row, col(kind, cj)],
                                           own_c.at[kind], own_sem.at[2 + kind]))
    for copy in loads:
        copy.start()
    pl.semaphore_wait(barrier, count)

    def remote(a, b, s, r, peer):
        copy = pltpu.make_async_remote_copy(
            src_ref=a, dst_ref=b, send_sem=s, recv_sem=r, device_id=peer, device_id_type=MESH
        )
        copy.start()
        return copy

    def done(ref, sem):
        pltpu.make_async_copy(ref, ref, sem).wait()

    first, second, third, fourth = {}, {}, {}, {}

    def p1(k):
        j, d, h = units[k]
        first[k] = (
            remote(src.at[1 - x, :, d, :, :, row(h), col(0, j)], r1a.at[k],
                   p1s.at[0], p1r.at[0, k], x_peer),
            remote(src.at[:, :, d, :, 1 - y, row(h), col(1, j)], r1b.at[k],
                   p1s.at[1], p1r.at[1, k], y_peer),
        )

    def two_a(k, core, side):
        j, d, h = units[k]
        own = own_a[core, d, :, side, row(h), pl.ds(j * cw, cw)]
        return own.astype(F32) + r1a[k, core, :, side].astype(F32)

    def two_b(k, core, side):
        j, d, h = units[k]
        own = own_b[side, core, d, :, row(h), pl.ds(j * cw, cw)]
        return own.astype(F32) + r1b[k, side, core].astype(F32)

    def q1(k):
        a, b = first[k]
        a.wait_recv()
        for side in range(2):
            s1a[k, side] = two_a(k, 1 - c, side)
        ca = remote(s1a.at[k], r2a.at[k], q1s.at[0], q1r.at[0, k], c_peer)
        b.wait_recv()
        for side in range(2):
            s1b[k, side] = two_b(k, 1 - c, side)
        cb = remote(s1b.at[k], r2b.at[k], q1s.at[1], q1r.at[1, k], c_peer)
        second[k] = (ca, cb)

    def p2(k):
        a, b = second[k]
        a.wait_recv()
        s2[0, k] = two_a(k, c, 1 - y) + r2a[k, 1 - y]
        ca = remote(s2.at[0, k], r3.at[0, k], p2s.at[0], p2r.at[0, k], y_peer)
        b.wait_recv()
        s2[1, k] = two_b(k, c, 1 - x) + r2b[k, 1 - x]
        cb = remote(s2.at[1, k], r3.at[1, k], p2s.at[1], p2r.at[1, k], x_peer)
        third[k] = (ca, cb)

    def p3(k):
        copies = []
        for kind in range(2):
            third[k][kind].wait_recv()
            if kind == 0:
                s3[0, k] = two_a(k, c, y) + r2a[k, y] + r3[0, k]
            else:
                s3[1, k] = two_b(k, c, x) + r2b[k, x] + r3[1, k]
            for o in range(1, nz):
                to = lax.rem(z + o, nz)
                copies.append(remote(s3.at[kind, k, to], r4.at[kind, k, z],
                                     p3s.at[kind], p3r.at[kind, k], z_peer(o)))
        fourth[k] = copies

    z_first, z_core, z_last = [], [], []

    def c_z():
        for kind in range(2):
            for o in range(1, nz):
                to = lax.rem(z + o, nz)
                z_first.append(remote(src.at[:, :, cd, to, :, c_row, col(kind, cj)], rz.at[kind, o - 1],
                                      zs.at[kind], zr.at[kind], z_peer(o)))

    def c_sum(kind, core, side):
        total = own_c[kind, side, core].astype(F32)
        for o in range(1, nz):
            total = total + rz[kind, o - 1, side, core].astype(F32)
        return total

    def c_core():
        for kind in range(2):
            done(rz.at[kind], zr.at[kind])
            for side in range(2):
                sc[kind, side] = c_sum(kind, 1 - c, side)
            z_core.append(remote(sc.at[kind], rc.at[kind], cs.at[kind], cr.at[kind], c_peer))

    def c_xy():
        for kind in range(2):
            z_core[kind].wait_recv()
            for side in range(2):
                tc[kind, side] = c_sum(kind, c, side) + rc[kind, side]
            for i, (a, b, peer) in enumerate(
                [(1 - x, 1 - y, d_peer), (1 - x, y, x_peer), (x, 1 - y, y_peer)]
            ):
                z_last.append(remote(tc.at[kind, a, b], rd.at[kind, i], ds.at[kind], dr.at[kind], peer))

    scale = 1.0 / jnp.sqrt(F32(groups * members))

    def halo(side, a, b):
        there, peer = beside[side]

        @pl.when(there)
        def _():
            remote(a, b, hs.at[side], hr.at[side], peer)

    def finish(kind, unit, total):
        j, d, h = unit
        cols = col(kind, j)
        span = pl.ds(h, total.shape[0])
        img[d, span, cols] = total * scale
        if d == 0:
            halo(0, img.at[d, span, cols], high.at[span, cols])
        if d == nd - 1:
            halo(1, img.at[d, span, cols], low.at[span, cols])
        if h == 0:
            halo(2, img.at[d, pl.ds(0, edge), cols], bottom.at[d, :, cols])
        if h + total.shape[0] == rows:
            halo(3, img.at[d, pl.ds(rows - edge, edge), cols], top.at[d, :, cols])

    def last(k):
        for kind in range(2):
            total = s3[kind, k, z]
            done(r4.at[kind, k, pl.ds(0, nz - 1)], p3r.at[kind, k])
            for o in range(1, nz):
                total = total + r4[kind, k, lax.rem(z + nz - o, nz)]
            finish(kind, units[k], total)

    def c_last():
        for kind in range(2):
            total = tc[kind, x, y]
            done(rd.at[kind], dr.at[kind])
            for i in range(3):
                total = total + rd[kind, i]
            finish(kind, c_unit, total)

    ahead, lag2, lag3, lag4 = 3, 0, 2, 4
    at_core = min(3, steps - 1)
    at_xy = max(steps - 2, at_core)
    p1(0)
    c_z()
    for k in range(1, min(ahead, steps)):
        p1(k)
    for copy in loads:
        copy.wait()
    for k in range(steps + lag4):
        if k < steps:
            q1(k)
        if 0 <= k - lag2 < steps:
            p2(k - lag2)
        if k + ahead < steps:
            p1(k + ahead)
        if 0 <= k - lag3 < steps:
            p3(k - lag3)
        if k == at_core:
            c_core()
        if k == at_xy:
            c_xy()
        if k == steps + lag4 - 1:
            c_last()
        if 0 <= k - lag4 < steps:
            last(k - lag4)
    for side, ref in enumerate([high, low, bottom, top]):
        @pl.when(beside[side ^ 1][0])
        def _():
            done(ref, hr.at[side])

    rown = lax.broadcasted_iota(jnp.int32, (rows, width), 0)
    coln = lax.broadcasted_iota(jnp.int32, (rows, width), 1)
    for d in range(nd):
        here = img[d]
        below = img[d - 1] if d > 0 else jnp.where(g > 0, low[...], 0.0)
        above = img[d + 1] if d < nd - 1 else jnp.where(g < groups - 1, high[...], 0.0)
        before = jnp.where(t > 0, top[d, edge - 1:edge, :], 0.0)
        after = jnp.where(t < members - 1, bottom[d, 0:1, :], 0.0)
        near = above + below
        near = near + jnp.where(rown == rows - 1, after, pltpu.roll(here, rows - 1, 0))
        near = near + jnp.where(rown == 0, before, pltpu.roll(here, 1, 0))
        near = near + jnp.where(coln == width - 1, 0.0, pltpu.roll(here, width - 1, 1))
        near = near + jnp.where(coln == 0, 0.0, pltpu.roll(here, 1, 1))
        out[d] = 6.0 * here - near
    for side, ref in enumerate([high, low, bottom, top]):
        @pl.when(beside[side][0])
        def _():
            done(ref, hs.at[side])
    for kind, (one, two) in enumerate([(r1a, r2a), (r1b, r2b)]):
        done(one, p1s.at[kind])
        done(two, q1s.at[kind])
        done(r3.at[kind], p2s.at[kind])
        done(r4.at[kind, :, pl.ds(0, nz - 1)], p3s.at[kind])
        done(rz.at[kind], zs.at[kind])
        done(rc.at[kind], cs.at[kind])
        done(rd.at[kind], ds.at[kind])


def body(groups, members, partials):
    shots, depth, lateral, width = partials.shape
    nd, nz, rows, cw = depth // groups, members // 2, lateral // members, width // 4
    parts = 2 if rows % 32 == 0 else 1
    rr, edge = rows // parts, min(8, rows)
    crows = rr
    steps = 2 * nd * parts - crows // rr
    src = partials.reshape(2, 2, nd, nz, 2, rows, width)
    kind = partials.dtype
    dma = pltpu.SemaphoreType.DMA
    return pl.pallas_call(
        functools.partial(kernel, groups, members),
        out_shape=jax.ShapeDtypeStruct((nd, rows, width), F32),
        in_specs=[pl.BlockSpec(memory_space=pl.ANY)],
        out_specs=pl.BlockSpec(memory_space=pltpu.VMEM),
        scratch_shapes=[
            pltpu.VMEM((2, nd, nz, 2, rows, 2 * cw), kind),
            pltpu.VMEM((2, 2, nd, nz, rows, 2 * cw), kind),
            pltpu.VMEM((2, 2, 2, 2, crows, cw), kind),
            pltpu.VMEM((steps, 2, nz, 2, rr, cw), kind),
            pltpu.VMEM((steps, 2, 2, nz, rr, cw), kind),
            pltpu.VMEM((steps, 2, nz, rr, cw), F32),
            pltpu.VMEM((steps, 2, nz, rr, cw), F32),
            pltpu.VMEM((steps, 2, nz, rr, cw), F32),
            pltpu.VMEM((steps, 2, nz, rr, cw), F32),
            pltpu.VMEM((2, steps, nz, rr, cw), F32),
            pltpu.VMEM((2, steps, nz, rr, cw), F32),
            pltpu.VMEM((2, steps, nz, rr, cw), F32),
            pltpu.VMEM((2, steps, nz, rr, cw), F32),
            pltpu.VMEM((2, nz - 1, 2, 2, 2, crows, cw), kind),
            pltpu.VMEM((2, 2, 2, crows, cw), F32),
            pltpu.VMEM((2, 2, 2, crows, cw), F32),
            pltpu.VMEM((2, 2, 2, crows, cw), F32),
            pltpu.VMEM((2, 3, crows, cw), F32),
            pltpu.VMEM((nd, rows, width), F32),
            pltpu.VMEM((rows, width), F32),
            pltpu.VMEM((rows, width), F32),
            pltpu.VMEM((nd, edge, width), F32),
            pltpu.VMEM((nd, edge, width), F32),
            dma((4,)),
            dma((2,)), dma((2, steps)),
            dma((2,)), dma((2, steps)),
            dma((2,)), dma((2, steps)),
            dma((2,)), dma((2, steps)),
            dma((2,)), dma((2,)),
            dma((2,)), dma((2,)),
            dma((2,)), dma((2,)),
            dma((4,)), dma((4,)),
        ],
        compiler_params=pltpu.CompilerParams(collective_id=0, has_side_effects=True),
    )(src)


def solution(mesh):
    groups, members = mesh.shape["shot"], mesh.shape["tile"]
    return jax.shard_map(
        functools.partial(body, groups, members),
        mesh=mesh,
        in_specs=(P(("shot", "tile"), None, None, None),),
        out_specs=P("shot", "tile", None),
        check_vma=False,
    )
```

time: 53.8 us -> 51.5 us (0.957)
  Pallas kernels: 51.9 us -> 49.7 us
    pallas_call x1, Pallas kernels: 51.9 us -> 49.7 us  [body(): pl.pallas_call(functools.partial(kernel, groups, members), out_shape=jax....]
where the time goes in v3:
time: 51.5 us; the launch traced here: 51.3 us
  Pallas kernels  49.7 us (97%)
  local copies, waits for them, and re-layouts  1.67 us (3%)
    pallas_call x1, Pallas kernels, body(): pl.pallas_call(functools.partial(kernel, groups, members), out_shape=jax....  49.7 us
    unnamed x1, local copies, waits for them, and re-layouts  1.67 us

profile of v3, /device:TPU:0, one launch (start us, length us, event | category | flops | bytes accessed | tf_op | source)
XLA Modules:
  0.0 51.3 jit_solution(10763607212058651974)
XLA Ops:
  0.0 49.7 %shard_map.17 = f32[2,64,512]{2,1,0:T(8,128)} custom-call(bf16[2,2,2,4,2,64,512]{6,5,4,3,2,1,0:T(8,128)(2,1)} %bitcast.1), custom_call_target="tpu_custom_call" | custom-call | tf_op jit(solution)/shard_map/pallas_call | solution.py:287
  49.7 1.7 %copy.3 = f32[2,64,512]{2,1,0:T(8,128)} copy(f32[2,64,512]{2,1,0:T(8,128)} %shard_map.17) | data formatting | bytes 524288

commit v4 on v3

--- a/solution.py
+++ b/solution.py
@@ -215,8 +215,8 @@
                 total = total + rd[kind, i]
             finish(kind, c_unit, total)
 
-    ahead, lag2, lag3, lag4 = 3, 0, 2, 4
-    at_core = min(3, steps - 1)
+    ahead, lag2, lag3, lag4 = 3, 0, 3, 7
+    at_core = min(6, steps - 1)
     at_xy = max(steps - 2, at_core)
     p1(0)
     c_z()
@@ -277,9 +277,9 @@
 def body(groups, members, partials):
     shots, depth, lateral, width = partials.shape
     nd, nz, rows, cw = depth // groups, members // 2, lateral // members, width // 4
-    parts = 2 if rows % 32 == 0 else 1
+    parts = 4 if rows % 64 == 0 else 1
     rr, edge = rows // parts, min(8, rows)
-    crows = rr
+    crows = 2 * rr if parts > 1 else rr
     steps = 2 * nd * parts - crows // rr
     src = partials.reshape(2, 2, nd, nz, 2, rows, width)
     kind = partials.dtype

time: 51.5 us -> 49.4 us (0.959)
  Pallas kernels: 49.7 us -> 47.5 us
    pallas_call x1, Pallas kernels: 49.7 us -> 47.5 us  [body(): pl.pallas_call(functools.partial(kernel, groups, members), out_shape=jax....]
where the time goes in v4:
time: 49.4 us; the launch traced here: 49.2 us
  Pallas kernels  47.5 us (96%)
  local copies, waits for them, and re-layouts  1.67 us (3%)
    pallas_call x1, Pallas kernels, body(): pl.pallas_call(functools.partial(kernel, groups, members), out_shape=jax....  47.5 us
    unnamed x1, local copies, waits for them, and re-layouts  1.67 us

profile of v4, /device:TPU:0, one launch (start us, length us, event | category | flops | bytes accessed | tf_op | source)
XLA Modules:
  0.0 49.2 jit_solution(1086494748734624092)
XLA Ops:
  0.0 47.5 %shard_map.17 = f32[2,64,512]{2,1,0:T(8,128)} custom-call(bf16[2,2,2,4,2,64,512]{6,5,4,3,2,1,0:T(8,128)(2,1)} %bitcast.1), custom_call_target="tpu_custom_call" | custom-call | tf_op jit(solution)/shard_map/pallas_call | solution.py:287
  47.5 1.7 %copy.3 = f32[2,64,512]{2,1,0:T(8,128)} copy(f32[2,64,512]{2,1,0:T(8,128)} %shard_map.17) | data formatting | bytes 524288
